TPU v7x, 32 devices: a whole 2x2x4 slice. The times are simulated.
32 devices in a mesh: dp: 8 (over y, x, core), fsdp: 4 (over z).
Axes of the slice: x: 2, y: 2, z: 4, core: 2. Of those that a mesh axis runs over, the one named last changes fastest.
Arguments:
- tokens: bfloat16 [64, 512, 768], P(('dp', 'fsdp')), may hold values from -6 to 6
- lengths: int32 [64], P(('dp', 'fsdp')), may hold values from 1 to 512, 24576 in all
- cotangent: bfloat16 [64, 512, 768], P(('dp', 'fsdp')), may hold values from -6 to 6
- w_query: bfloat16 [768, 768], P(('dp', 'fsdp')), may hold values from -0.21875 to 0.21875
- w_key: bfloat16 [768, 768], P(('dp', 'fsdp')), may hold values from -0.21875 to 0.21875
- w_value: bfloat16 [768, 768], P(('dp', 'fsdp')), may hold values from -0.21875 to 0.21875
- w_out: bfloat16 [768, 768], P(('dp', 'fsdp')), may hold values from -0.875 to 0.875
- w_up: bfloat16 [768, 3072], P(('dp', 'fsdp')), may hold values from -0.21875 to 0.21875
- w_down: bfloat16 [3072, 768], P(('dp', 'fsdp')), may hold values from -0.109375 to 0.109375
- shared_a: bfloat16 [768, 1024], P(('dp', 'fsdp')), may hold values from -0.21875 to 0.21875
- shared_b: bfloat16 [1024, 768], P(('dp', 'fsdp')), may hold values from -0.1875 to 0.1875
- gain_one: float32 [768], replicated, may hold values from 0.5 to 1.5
- gain_two: float32 [768], replicated, may hold values from 0.5 to 1.5
- query_d: float32 [1024], replicated, may hold values from -4 to 4
- query_b: float32 [768], replicated, may hold values from -4 to 4
- value_d: float32 [1024], replicated, may hold values from -4 to 4
- value_b: float32 [768], replicated, may hold values from -4 to 4
Outputs:
- output: bfloat16 [64, 512, 768], P(('dp', 'fsdp'))
- grad_tokens: bfloat16 [64, 512, 768], P(('dp', 'fsdp'))
- grad_query_d: float32 [1024], replicated
- grad_query_b: float32 [768], replicated
- grad_value_d: float32 [1024], replicated
- grad_value_b: float32 [768], replicated
- rank_stats: float32 [1024], replicated
Inputs may be any that keep to these rules, and one draw needn't show every extreme that they name: The 64 lengths sum to 24576, and the largest equals 512.
All inputs are finite; a program needn't handle non-finite values. No bound on the sum of `lengths` on one device may be relied on, other than what follows from the above.
Results may differ from a plain program's by a relative error of at most 0.015.
The roundings to bfloat16 on the way count: a program that leaves them out, or rounds other values in their place, can miss the bound.
Values may be sent and summed in bfloat16 or wider, within the bound.
A program may use at most 192 MiB of HBM per device.

v0:
```python
import jax
import jax.numpy as jnp
from jax import lax
from jax.sharding import PartitionSpec as P

D = 768
H = 12
HD = 64
L = 512
SEQ_DEV = 2


eps_norm = 1e-05
neg_fill = -1000000000.0


def layer_norm(hidden, gain):
    center = jnp.mean(hidden, axis=-1, keepdims=True)
    shifted = hidden - center
    spread = jnp.mean(shifted * shifted, axis=-1, keepdims=True)
    return shifted * lax.rsqrt(spread + eps_norm) * gain


def exact_gelu(pre_act):
    return jax.nn.gelu(pre_act, approximate=False)


def dot_plain(left, right):
    return jnp.dot(left, right, preferred_element_type=jnp.float32)


def dot_trans(left, right):
    return lax.dot_general(
        left, right, (((1,), (1,)), ((), ())), preferred_element_type=jnp.float32
    )


def split_heads(row_data):
    return row_data.reshape(SEQ_DEV, L, H, HD).transpose(0, 2, 1, 3).reshape(SEQ_DEV * H, L, HD)


def join_heads(head_data):
    return head_data.reshape(SEQ_DEV, H, L, HD).transpose(0, 2, 1, 3).reshape(SEQ_DEV * L, D)


def shards(
    tokens,
    lengths,
    cotangent,
    w_query,
    w_key,
    w_value,
    w_out,
    w_up,
    w_down,
    shared_a,
    shared_b,
    gain_one,
    gain_two,
    query_d,
    query_b,
    value_d,
    value_b,
):
    row_count = SEQ_DEV * L
    head_scale = HD ** (-0.5)
    local_mats = (w_query, w_key, w_value, w_out, w_up, w_down, shared_a, shared_b)
    full_mats = (
        lax.all_gather(local_mats[0], ("dp", "fsdp"), axis=0, tiled=True),
        lax.all_gather(local_mats[1], ("dp", "fsdp"), axis=0, tiled=True),
        lax.all_gather(local_mats[2], ("dp", "fsdp"), axis=0, tiled=True),
        lax.all_gather(local_mats[3], ("dp", "fsdp"), axis=0, tiled=True),
        lax.all_gather(local_mats[4], ("dp", "fsdp"), axis=0, tiled=True),
        lax.all_gather(local_mats[5], ("dp", "fsdp"), axis=0, tiled=True),
        lax.all_gather(local_mats[6], ("dp", "fsdp"), axis=0, tiled=True),
        lax.all_gather(local_mats[7], ("dp", "fsdp"), axis=0, tiled=True),
    )
    wq, wk, wv, wo, wu, wd, mat_a, mat_b = full_mats
    inputs = tokens.reshape(row_count, D)
    positions = lax.broadcasted_iota(jnp.int32, (SEQ_DEV, L), 1)
    live = (positions < lengths[:, None]).astype(jnp.float32)
    live_rows = live.reshape(row_count, 1)
    key_live = jnp.repeat(live, H, axis=0)
    rank_act = dot_plain(inputs, mat_a)
    square_sum = jnp.sum(rank_act * rank_act * live_rows, axis=0)
    count = jnp.sum(lengths).astype(jnp.float32)
    total_square, total_count = lax.psum((square_sum, count), ("dp", "fsdp"))
    rank_q = (rank_act * query_d).astype(jnp.bfloat16)
    rank_v = (rank_act * value_d).astype(jnp.bfloat16)
    delta_q = dot_plain(rank_q, mat_b)
    delta_v = dot_plain(rank_v, mat_b)
    queries = (dot_plain(inputs, wq) + query_b * delta_q).astype(jnp.bfloat16)
    key_rows = dot_plain(inputs, wk).astype(jnp.bfloat16)
    values = (dot_plain(inputs, wv) + value_b * delta_v).astype(jnp.bfloat16)
    q_heads = split_heads(queries)
    k_heads = split_heads(key_rows)
    v_heads = split_heads(values)

    def attend_block(pieces):
        q_blk, k_blk, v_blk, live_keys = pieces
        scores = (
            jnp.einsum("qd,kd->qk", q_blk, k_blk, preferred_element_type=jnp.float32) * head_scale
        )
        scores = jnp.where(live_keys[None, :] > 0, scores, neg_fill)
        row_max = jnp.max(scores, axis=-1, keepdims=True)
        log_total = row_max + jnp.log(jnp.sum(jnp.exp(scores - row_max), axis=-1, keepdims=True))
        probs = jnp.exp(scores - log_total).astype(jnp.bfloat16)
        context = jnp.dot(probs, v_blk, preferred_element_type=jnp.float32).astype(jnp.bfloat16)
        return (context, log_total[:, 0])

    ctx_heads, log_totals = lax.map(attend_block, (q_heads, k_heads, v_heads, key_live))
    context = join_heads(ctx_heads)
    h_one = inputs + dot_plain(context, wo)
    x_one = layer_norm(h_one, gain_one)
    x_low = x_one.astype(jnp.bfloat16)

    def feed_block(block):
        act = exact_gelu(dot_plain(block, wu)).astype(jnp.bfloat16)
        return dot_plain(act, wd)

    x_blocks = x_low.reshape(SEQ_DEV, L, D)
    ffn_out = lax.map(feed_block, x_blocks).reshape(row_count, D)
    h_two = x_one + ffn_out
    output = layer_norm(h_two, gain_two)
    cot_rows = cotangent.reshape(row_count, D).astype(jnp.float32) * live_rows
    _, norm_two_back = jax.vjp(lambda hidden: layer_norm(hidden, gain_two), h_two)
    g_h2 = norm_two_back(cot_rows)[0]
    back_mats = (
        lax.all_gather(local_mats[0], ("dp", "fsdp"), axis=0, tiled=True),
        lax.all_gather(local_mats[1], ("dp", "fsdp"), axis=0, tiled=True),
        lax.all_gather(local_mats[2], ("dp", "fsdp"), axis=0, tiled=True),
        lax.all_gather(local_mats[3], ("dp", "fsdp"), axis=0, tiled=True),
        lax.all_gather(local_mats[4], ("dp", "fsdp"), axis=0, tiled=True),
        lax.all_gather(local_mats[5], ("dp", "fsdp"), axis=0, tiled=True),
        lax.all_gather(local_mats[6], ("dp", "fsdp"), axis=0, tiled=True),
        lax.all_gather(local_mats[7], ("dp", "fsdp"), axis=0, tiled=True),
    )
    bq_mat, bk_mat, bv_mat, bo_mat, bu_mat, bd_mat, back_a, back_b = back_mats
    g_ffn = g_h2.astype(jnp.bfloat16)

    def feed_back(pieces):
        block, grad_out = pieces
        pre_act = dot_plain(block, bu_mat)
        g_act = dot_trans(grad_out, bd_mat)
        _, gelu_back = jax.vjp(exact_gelu, pre_act)
        g_pre = gelu_back(g_act)[0].astype(jnp.bfloat16)
        return dot_trans(g_pre, bu_mat)

    g_x1 = g_h2 + lax.map(feed_back, (x_blocks, g_ffn.reshape(SEQ_DEV, L, D))).reshape(row_count, D)
    _, norm_one_back = jax.vjp(lambda hidden: layer_norm(hidden, gain_one), h_one)
    g_h1 = norm_one_back(g_x1)[0]
    g_attn = g_h1.astype(jnp.bfloat16)
    g_context = dot_trans(g_attn, bo_mat).astype(jnp.bfloat16)
    gc_heads = split_heads(g_context)

    def attend_back(pieces):
        q_blk, k_blk, v_blk, live_keys, log_total, gc_blk = pieces
        scores = (
            jnp.einsum("qd,kd->qk", q_blk, k_blk, preferred_element_type=jnp.float32) * head_scale
        )
        scores = jnp.where(live_keys[None, :] > 0, scores, neg_fill)
        probs = jnp.exp(scores - log_total[:, None])
        probs_low = probs.astype(jnp.bfloat16)
        g_probs = jnp.einsum("qd,kd->qk", gc_blk, v_blk, preferred_element_type=jnp.float32)
        g_scores = (probs * (g_probs - jnp.sum(g_probs * probs, axis=-1, keepdims=True))).astype(
            jnp.bfloat16
        )
        g_q = (jnp.dot(g_scores, k_blk, preferred_element_type=jnp.float32) * head_scale).astype(
            jnp.bfloat16
        )
        g_k = (
            jnp.einsum("qk,qd->kd", g_scores, q_blk, preferred_element_type=jnp.float32)
            * head_scale
        ).astype(jnp.bfloat16)
        g_v = jnp.einsum("qk,qd->kd", probs_low, gc_blk, preferred_element_type=jnp.float32).astype(
            jnp.bfloat16
        )
        return (g_q, g_k, g_v)

    gq_heads, gk_heads, gv_heads = lax.map(
        attend_back, (q_heads, k_heads, v_heads, key_live, log_totals, gc_heads)
    )
    g_queries = join_heads(gq_heads)
    g_keys = join_heads(gk_heads)
    g_values = join_heads(gv_heads)
    gq_wide = g_queries.astype(jnp.float32)
    gv_wide = g_values.astype(jnp.float32)
    grad_qb = jnp.sum(gq_wide * delta_q, axis=0)
    grad_vb = jnp.sum(gv_wide * delta_v, axis=0)
    g_dq = (query_b * gq_wide).astype(jnp.bfloat16)
    g_dv = (value_b * gv_wide).astype(jnp.bfloat16)
    t_q = dot_trans(g_dq, back_b)
    t_v = dot_trans(g_dv, back_b)
    grad_qd = jnp.sum(t_q * rank_act, axis=0)
    grad_vd = jnp.sum(t_v * rank_act, axis=0)
    g_rank = (t_q * query_d + t_v * value_d).astype(jnp.bfloat16)
    g_inputs = (
        g_h1
        + dot_trans(g_queries, bq_mat)
        + dot_trans(g_keys, bk_mat)
        + dot_trans(g_values, bv_mat)
        + dot_trans(g_rank, back_a)
    )
    sum_qd, sum_qb, sum_vd, sum_vb = lax.psum((grad_qd, grad_qb, grad_vd, grad_vb), ("dp", "fsdp"))
    rank_stats = total_square / total_count
    output_out = output.astype(jnp.bfloat16).reshape(SEQ_DEV, L, D)
    grad_tokens = g_inputs.astype(jnp.bfloat16).reshape(SEQ_DEV, L, D)
    return (output_out, grad_tokens, sum_qd, sum_qb, sum_vd, sum_vb, rank_stats)


def solution(mesh):
    in_specs = (
        P(("dp", "fsdp"), None, None),
        P(("dp", "fsdp")),
        P(("dp", "fsdp"), None, None),
        P(("dp", "fsdp"), None),
        P(("dp", "fsdp"), None),
        P(("dp", "fsdp"), None),
        P(("dp", "fsdp"), None),
        P(("dp", "fsdp"), None),
        P(("dp", "fsdp"), None),
        P(("dp", "fsdp"), None),
        P(("dp", "fsdp"), None),
        P(),
        P(),
        P(),
        P(),
        P(),
        P(),
    )
    out_specs = (
        P(("dp", "fsdp"), None, None),
        P(("dp", "fsdp"), None, None),
        P(),
        P(),
        P(),
        P(),
        P(),
    )
    return jax.shard_map(shards, mesh=mesh, in_specs=in_specs, out_specs=out_specs, check_vma=False)
```

profile of v0, /device:TPU:0, one launch (start us, length us, event | category | flops | bytes accessed | tf_op | source)
XLA Modules:
  0.0 919.7 jit_solution(1533905239916311515)
XLA Ops:
  15.9 51.6 %all-gather.15.cloned.1.call-done = bf16[768,768]{1,0:T(8,128)(2,1)} async-done(((bf16[24,768]{1,0:T(8,128)(2,1)}), bf16[768,768]{1,0:T(8,128)(2,1)}) %all-gather.15.cloned.1.call-update) | async-done | bytes 1179664 | tf_op jit(solution)/shard_map/all_gather | solution.py:70
  67.5 3.1 convolution_convert_fusion.3
  72.6 3.5 copy.62
  76.1 48.2 %all-gather.11.cloned.1.call-done = bf16[768,1024]{1,0:T(8,128)(2,1)} async-done(((bf16[24,1024]{1,0:T(8,128)(2,1)}), bf16[768,1024]{1,0:T(8,128)(2,1)}) %all-gather.11.cloned.1.call-update) | async-done | bytes 1572880 | tf_op jit(solution)/shard_map/all_gather | solution.py:75
  124.3 5.1 fusion.191
  129.5 51.7 %all-gather.13.cloned.1.call-done = bf16[1024,768]{1,0:T(8,128)(2,1)} async-done(((bf16[32,768]{1,0:T(8,128)(2,1)}), bf16[1024,768]{1,0:T(8,128)(2,1)}) %all-gather.13.cloned.1.call-update) | async-done | bytes 1572880 | tf_op jit(solution)/shard_map/all_gather | solution.py:76
  181.1 4.5 fusion.169
  185.6 51.1 %all-gather.9.cloned.1.call-done = bf16[768,768]{1,0:T(8,128)(2,1)} async-done(((bf16[24,768]{1,0:T(8,128)(2,1)}), bf16[768,768]{1,0:T(8,128)(2,1)}) %all-gather.9.cloned.1.call-update) | async-done | bytes 1179664 | tf_op jit(solution)/shard_map/all_gather | solution.py:69
  236.7 4.3 add_convert_fusion.3
  243.9 3.4 copy.61
  247.4 4.5 fusion.170
  251.9 40.4 %all-gather.17.cloned.1.call-done = bf16[768,768]{1,0:T(8,128)(2,1)} async-done(((bf16[24,768]{1,0:T(8,128)(2,1)}), bf16[768,768]{1,0:T(8,128)(2,1)}) %all-gather.17.cloned.1.call-update) | async-done | bytes 1179664 | tf_op jit(solution)/shard_map/all_gather | solution.py:71
  292.3 4.3 add_convert_fusion.2
  298.3 2.4 reshape.197
  300.7 4.1 copy.63
  306.1 105.4 %while.46 = (s32[]{:T(128)}, bf16[24,512,64]{1,2,0:T(8,128)(2,1)}, f32[24,512]{1,0:T(8,128)}, f32[24,512]{1,0:T(8,128)S(1)}, bf16[24,512,64]{2,1,0:T(8,128)(2,1)...) while((s32[]{:T(128)}, bf16[24,512,64]{1,2,0:T(8,128)(2,1)}, ...), condition=%wide.region_3.0_spmd, body=%wide.region_0.3_spmd.sunk | while | flops 68976640 | bytes 3628133 | solution.py:111
  411.6 4.2 copy.49
  417.3 3.8 fusion.190
  425.0 53.0 %all-gather.23.cloned.1.call-done = bf16[3072,768]{1,0:T(8,128)(2,1)} async-done(((bf16[96,768]{1,0:T(8,128)(2,1)}), bf16[3072,768]{1,0:T(8,128)(2,1)}) %all-gather.23.cloned.1.call-update) | async-done | bytes 4718608 | tf_op jit(solution)/shard_map/all_gather | solution.py:74
  478.1 1.8 broadcast.294.clone
  479.9 44.2 %while.47 = (s32[]{:T(128)}, f32[2,512,768]{2,1,0:T(8,128)}, bf16[2,512,768]{2,1,0:T(8,128)(2,1)}, bf16[768,3072]{1,0:T(8,128)(2,1)}, bf16[3072,768]{1,0:T(8,128)(2,1)}, /*index=5*/s32[]{:T(128)}) while((s32[]{:T(128)}, f32[2,512,768]{2,1,0:T(8,128)}, bf16[2,512,768]{2,1,0:T(8,128)(2,1)}, bf16[768,3072]{1,0:T(8,128)(2,1)}, ...), condition=%wide.region_7.8_spmd, body=%wide.region_6.7_spmd.sunk | while | flops 4934074368 | bytes 11797573 | solution.py:122
  479.9 22.0 %bitcast_dynamic-update-slice_fusion.4 = f32[2,512,768]{2,1,0:T(8,128)} fusion(f32[2,512,768]{2,1,0:T(8,128)} %get-tuple-element.483, s32[]{:T(128)} %get-tuple-element.482, bf16[3072,768]{1,0:T(8,128)(2,1)} %get-tuple-element.492, bf16[768,3072]{1,0:T(8,128)(2,1)} %get-tuple-element.491, bf16[2,512,768]{2,1,0:T(8,128)(2,1)} %get-tuple-element.490), kind=kOutput, calls=%fused_computation.20.clone.1 | convolution fusion | flops 4934074368 | bytes 11797504 | tf_op jit(solution)/shard_map/while/body/eval_jaxpr/dot_general | solution.py:29
  501.9 21.8 %bitcast_dynamic-update-slice_fusion.4 = f32[2,512,768]{2,1,0:T(8,128)} fusion(f32[2,512,768]{2,1,0:T(8,128)} %get-tuple-element.483, s32[]{:T(128)} %get-tuple-element.482, bf16[3072,768]{1,0:T(8,128)(2,1)} %get-tuple-element.492, bf16[768,3072]{1,0:T(8,128)(2,1)} %get-tuple-element.491, bf16[2,512,768]{2,1,0:T(8,128)(2,1)} %get-tuple-element.490), kind=kOutput, calls=%fused_computation.20.clone.1 | convolution fusion | flops 4934074368 | bytes 11797504 | tf_op jit(solution)/shard_map/while/body/eval_jaxpr/dot_general | solution.py:29
  524.2 2.8 fusion.188
  528.4 2.8 fusion.187
  532.8 1.8 broadcast.294
  534.7 67.9 %while.48 = (s32[]{:T(128)}, f32[2,512,768]{2,1,0:T(8,128)}, bf16[2,512,768]{2,1,0:T(8,128)(2,1)}, bf16[768,3072]{1,0:T(8,128)(2,1)}, bf16[2,512,768]{2,1,0:T(8,128)(2,1)}, /*index=5*/bf16[3072,768]{1,0:T(8,128)(2,1)}, s32[]{:T(128)}) while((s32[]{:T(128)}, f32[2,512,768]{2,1,0:T(8,128)}, bf16[2,512,768]{2,1,0:T(8,128)(2,1)}, ...), condition=%wide.region_13.14_spmd, body=%wide.region_12.13_spmd.sunk | while | flops 7361003520 | bytes 29886028 | solution.py:149
  537.2 7.8 fusion.262
  545.1 24.7 %bitcast_dynamic-update-slice_fusion.5 = f32[2,512,768]{2,1,0:T(8,128)} fusion(f32[2,512,768]{2,1,0:T(8,128)} %get-tuple-element.502, s32[]{:T(128)} %get-tuple-element.501, bf16[768,3072]{1,0:T(8,128)(2,1)} %get-tuple-element.511, f32[512,3072]{1,0:T(8,128)} %fusion.262, bf16[3072,768]{1,0:T(8,128)(2,1)} %get-tuple-element.513, ...), kind=kOutput, calls=%fused_computation.77.clone.1 | convolution fusion | flops 4945084416 | bytes 18088960 | tf_op jit(solution)/shard_map/while/body/eval_jaxpr/dot_general | solution.py:33
  569.7 7.8 fusion.262
  577.6 24.6 %bitcast_dynamic-update-slice_fusion.5 = f32[2,512,768]{2,1,0:T(8,128)} fusion(f32[2,512,768]{2,1,0:T(8,128)} %get-tuple-element.502, s32[]{:T(128)} %get-tuple-element.501, bf16[768,3072]{1,0:T(8,128)(2,1)} %get-tuple-element.511, f32[512,3072]{1,0:T(8,128)} %fusion.262, bf16[3072,768]{1,0:T(8,128)(2,1)} %get-tuple-element.513, ...), kind=kOutput, calls=%fused_computation.77.clone.1 | convolution fusion | flops 4945084416 | bytes 18088960 | tf_op jit(solution)/shard_map/while/body/eval_jaxpr/dot_general | solution.py:33
  602.6 4.0 multiply_reduce_fusion.4
  607.3 1.8 fusion.186
  613.0 2.4 reshape.206
  615.4 4.1 copy.66
  623.6 211.6 %while.49 = (s32[]{:T(128)}, bf16[24,512,64]{1,2,0:T(8,128)(2,1)}, bf16[24,512,64]{1,2,0:T(8,128)(2,1)}, bf16[24,512,64]{1,2,0:T(8,128)(2,1)}, f32[24,512]{1,0:T...) while((s32[]{:T(128)}, bf16[24,512,64]{1,2,0:T(8,128)(2,1)}, ...), condition=%wide.region_18.19_spmd, body=%wide.region_16.18_spmd.sunk | while | flops 170295296 | bytes 8996981 | solution.py:180
  627.9 1.8 fusion.273
  636.7 1.8 fusion.273
  645.5 1.8 fusion.273
  680.8 1.8 fusion.273
  689.6 1.9 fusion.273
  698.4 1.8 fusion.273
  707.2 1.8 fusion.273
  716.1 1.8 fusion.273
  733.7 1.8 fusion.273
  742.5 1.8 fusion.273
  751.3 1.8 fusion.273
  760.1 1.8 fusion.273
  769.0 1.8 fusion.273
  777.8 1.8 fusion.273
  786.6 1.8 fusion.273
  813.0 1.8 fusion.273
  821.8 1.8 fusion.273
  830.7 1.8 fusion.273
  835.2 3.0 copy.56
  840.4 3.0 copy.58
  844.6 3.2 copy.57
  849.4 2.8 fusion.160
  852.2 1.8 fusion.178
  854.4 3.9 multiply_reduce_fusion.1
  858.3 39.8 %all-reduce = (f32[1024]{0:T(1024)}, f32[768]{0:T(1024)}, f32[1024]{0:T(1024)}, f32[768]{0:T(1024)}, f32[1024]{0:T(1024)S(1)}, /*index=5*/f32[]{:T(128)}) all-reduce(f32[1024]{0:T(1024)S(1)} %get-tuple-element.184, f32[768]{0:T(1024)S(1)} %get-tuple-element.267, ...), channel_id=1, replica_groups=mesh['dp'=8,'fsdp'=4] {'dp','fsdp'}, use_global_device_ids=true, to_apply=%region_20.21 | all-reduce | flops 4609 | bytes 36872 | tf_op jit(solution)/shard_map/psum | solution.py:204
  899.3 3.3 fusion.192
  903.6 3.4 fusion.171
  909.3 3.4 add_convert_fusion.1
  (472 shorter events, 311.5 us)
Async XLA Ops:
  7.2 60.3 %all-gather.15.cloned.1.call-start = ((), (), s32[]{:S(2)}) async-start(), calls=%async_computation.3 | async-start | bytes 1216512 | tf_op jit(solution)/shard_map/all_gather | solution.py:70
  7.9 116.4 %all-gather.11.cloned.1.call-start = ((), (), s32[]{:S(2)}) async-start(), calls=%async_computation.1 | async-start | bytes 1622016 | tf_op jit(solution)/shard_map/all_gather | solution.py:75
  8.6 172.5 %all-gather.13.cloned.1.call-start = ((), (), s32[]{:S(2)}) async-start(), calls=%async_computation.2 | async-start | bytes 1622016 | tf_op jit(solution)/shard_map/all_gather | solution.py:76
  9.4 227.4 %all-gather.9.cloned.1.call-start = ((), (), s32[]{:S(2)}) async-start(), calls=%async_computation | async-start | bytes 1216512 | tf_op jit(solution)/shard_map/all_gather | solution.py:69
  10.0 282.4 %all-gather.17.cloned.1.call-start = ((), (), s32[]{:S(2)}) async-start(), calls=%async_computation.4 | async-start | bytes 1216512 | tf_op jit(solution)/shard_map/all_gather | solution.py:71
  10.5 406.8 %all-gather.19.cloned.1.call-start = ((), (), s32[]{:S(2)}) async-start(), calls=%async_computation.5 | async-start | bytes 1216512 | tf_op jit(solution)/shard_map/all_gather | solution.py:72
  11.1 413.9 %all-gather.21.cloned.1.call-start = ((), (), s32[]{:S(2)}) async-start(), calls=%async_computation.6 | async-start | bytes 4866048 | tf_op jit(solution)/shard_map/all_gather | solution.py:73
  11.9 466.2 %all-gather.23.cloned.1.call-start = ((), (), s32[]{:S(2)}) async-start(), calls=%async_computation.7 | async-start | bytes 4866048 | tf_op jit(solution)/shard_map/all_gather | solution.py:74
  72.6 51.7 %copy-start.45 = (bf16[2,512,768]{2,1,0:T(8,128)(2,1)S(1)}, bf16[2,512,768]{2,1,0:T(8,128)(2,1)}, u32[]{:S(2)}) copy-start(bf16[2,512,768]{2,1,0:T(8,128)(2,1)} %param.25) | copy-start | bytes 4718596
  76.1 105.0 %copy-start.41 = (f32[1024]{0:T(1024)S(1)}, f32[1024]{0:T(1024)}, u32[]{:S(2)}) copy-start(f32[1024]{0:T(1024)} %param.38) | copy-start | bytes 12292
  129.5 107.3 %copy-start.48 = (f32[768]{0:T(1024)S(1)}, f32[768]{0:T(1024)}, u32[]{:S(2)}) copy-start(f32[768]{0:T(1024)} %param.39) | copy-start | bytes 9220
  185.6 51.1 %copy-start.16 = (f32[1024,768]{1,0:T(8,128)}, f32[1024,768]{1,0:T(8,128)S(1)}, u32[]{:S(2)}) copy-start(f32[1024,768]{1,0:T(8,128)S(1)} %fusion.169) | copy-start | bytes 9437188
  243.9 3.5 copy-start.43
  247.4 44.9 %copy-start.39 = (f32[768]{0:T(1024)S(1)}, f32[768]{0:T(1024)}, u32[]{:S(2)}) copy-start(f32[768]{0:T(1024)} %param.41) | copy-start | bytes 9220
  251.9 40.5 %copy-start.18 = (f32[1024,768]{1,0:T(8,128)}, f32[1024,768]{1,0:T(8,128)S(1)}, u32[]{:S(2)}) copy-start(f32[1024,768]{1,0:T(8,128)S(1)} %fusion.170) | copy-start | bytes 9437188
  411.5 5.8 copy-start.11
  411.6 5.8 copy-start.25
  421.2 1.7 copy-start
  421.2 2.2 copy-start.26
  421.2 1.6 copy-start.22
  421.7 0.6 copy-start.36
  422.8 0.6 copy-start.31
  479.9 44.2 %copy-start.1 = (f32[1024,768]{1,0:T(8,128)S(1)}, f32[1024,768]{1,0:T(8,128)}, u32[]{:S(2)}) copy-start(f32[1024,768]{1,0:T(8,128)} %copy-done) | copy-start | bytes 9437188
  479.9 44.2 %copy-start.23 = (f32[1024]{0:T(1024)S(1)}, f32[1024]{0:T(1024)}, u32[]{:S(2)}) copy-start(f32[1024]{0:T(1024)} %copy-done.22) | copy-start | bytes 12292
  479.9 44.2 %copy-start.27 = (f32[768]{0:T(1024)S(1)}, f32[768]{0:T(1024)}, u32[]{:S(2)}) copy-start(f32[768]{0:T(1024)} %param.36) | copy-start | bytes 9220
  479.9 44.2 %copy-start.32 = (f32[1024]{0:T(1024)S(1)}, f32[1024]{0:T(1024)}, u32[]{:S(2)}) copy-start(f32[1024]{0:T(1024)} %copy-done.31) | copy-start | bytes 12292
  524.1 2.8 copy-start.14
  524.2 2.8 copy-start.29
  524.2 2.8 copy-start.38
  531.2 3.4 copy-start.3
  531.2 3.4 copy-start.34
  534.6 67.9 %copy-start.2 = (f32[1024,768]{1,0:T(8,128)S(1)}, f32[1024,768]{1,0:T(8,128)}, u32[]{:S(2)}) copy-start(f32[1024,768]{1,0:T(8,128)} %copy-done) | copy-start | bytes 9437188
  534.6 67.9 %copy-start.24 = (f32[1024]{0:T(1024)S(1)}, f32[1024]{0:T(1024)}, u32[]{:S(2)}) copy-start(f32[1024]{0:T(1024)} %copy-done.22) | copy-start | bytes 12292
  534.6 67.9 %copy-start.28 = (f32[768]{0:T(1024)S(1)}, f32[768]{0:T(1024)}, u32[]{:S(2)}) copy-start(f32[768]{0:T(1024)} %param.36) | copy-start | bytes 9220
  534.6 67.9 %copy-start.35 = (f32[1024]{0:T(1024)S(1)}, f32[1024]{0:T(1024)}, u32[]{:S(2)}) copy-start(f32[1024]{0:T(1024)} %copy-done.34) | copy-start | bytes 12292
  602.6 4.0 copy-start.37
  602.6 4.0 copy-start.4
  602.6 4.7 copy-start.5
  602.6 4.7 copy-start.33
  607.3 3.5 copy-start.47
  609.2 1.7 copy-start.9
  838.7 4.8 copy-start.12
  844.6 4.9 copy-start.13
  844.6 4.9 copy-start.17
  849.4 2.8 copy-start.19
  849.4 2.8 copy-start.49
  852.2 2.2 copy-start.15
  852.2 2.2 copy-start.30
  852.2 2.2 copy-start.40
  854.4 3.9 copy-start.6
  899.3 3.4 copy-start.7
  899.3 4.3 copy-start.8
  899.3 4.3 copy-start.42
  899.3 4.3 copy-start.44
  903.6 3.4 copy-start.20
  903.6 3.5 copy-start.46
  907.1 1.9 copy-start.10
  907.1 2.2 copy-start.21
Sparse Core Ops, SparseCore 0:
  10.8 56.6 all-gather.14
  70.4 53.8 all-gather.10
  127.2 53.8 all-gather.12
  183.8 52.8 all-gather.8
  239.4 52.8 all-gather.16
  295.0 52.9 all-gather.18
  350.8 62.4 all-gather.20
  416.1 61.9 all-gather.22
where the time goes:
time: 935 us; the launch traced here: 920 us
  matrix products  380 us (41%)
  waiting for transfers between devices  301 us (32%)
  local copies, waits for them, and re-layouts  112 us (12%)
  other arithmetic  52 us (6%)
  blocking collectives  39.8 us (4%)
  loops' own time  18.5 us (2%)
  between operations  15.6 us (2%)
    dot_general x11, matrix products, dot_plain(): return jnp.dot(left, right, preferred_element_type=jnp.float32)  89.1 us
    dot_general x9, matrix products, dot_trans(): lax.dot_general(left, right, (((1,), (1,)), ((), ())), preferred_element_...  68.1 us
    all_gather x1, waiting for transfers between devices, shards(): lax.all_gather(local_mats[5], ('dp', 'fsdp'), axis=0, tiled=True)  53 us
    all_gather x1, waiting for transfers between devices, shards(): lax.all_gather(local_mats[7], ('dp', 'fsdp'), axis=0, tiled=True)  51.7 us
    all_gather x1, waiting for transfers between devices, shards(): lax.all_gather(local_mats[1], ('dp', 'fsdp'), axis=0, tiled=True)  51.6 us
    all_gather x1, waiting for transfers between devices, shards(): lax.all_gather(local_mats[0], ('dp', 'fsdp'), axis=0, tiled=True)  51.1 us
    all_gather x1, waiting for transfers between devices, shards(): lax.all_gather(local_mats[6], ('dp', 'fsdp'), axis=0, tiled=True)  48.2 us
    dot_general x24, matrix products, attend_back(): jnp.einsum('qk,qd->kd', g_scores, q_blk, preferred_element_type=jnp.float32)  43.9 us
  transfers between devices with their start and end apart: 8, of which 6 were waited for; matrix products, arithmetic and copies ran while one was open for 17% of the time, Pallas kernels for 0%

commit v1 on v0

v1 whole, which is shorter than its diff:
```python
import functools
import jax
import jax.numpy as jnp
from jax import lax
from jax.experimental import pallas as pl
from jax.experimental.pallas import tpu as pltpu

D = 768
H = 12
HD = 64
FF = 3072
R = 1024
L = 512
eps_norm = 1e-05
neg_fill = -1000000000.0
f32 = jnp.float32
bf16 = jnp.bfloat16


def mm(a, b):
    return jnp.dot(a, b, preferred_element_type=f32)


def mm_t(a, b):
    return lax.dot_general(a, b, (((1,), (1,)), ((), ())), preferred_element_type=f32)


def fold8(z):
    rows, cols = z.shape
    return jnp.sum(z.reshape(rows // 8, 8, cols), axis=0)


def vm(mib):
    return pltpu.CompilerParams(vmem_limit_bytes=mib << 20)


def proj_kernel(tm, len_ref, x_ref, w1_ref, b_ref, qd_ref, vd_ref, qb_ref, vb_ref,
                ra_ref, dq_ref, dv_ref, q_ref, k_ref, v_ref, sq_ref):
    i = pl.program_id(0)
    x = x_ref[...]
    ra = mm(x, w1_ref[:, :R])
    per_seq = L // tm
    length = len_ref[i // per_seq]
    pos = (i % per_seq) * tm + lax.broadcasted_iota(jnp.int32, (tm, 1), 0)
    live = (pos < length).astype(f32)

    @pl.when(i == 0)
    def _():
        sq_ref[...] = jnp.zeros_like(sq_ref)

    sq_ref[...] += fold8(ra * ra * live)
    ra_ref[...] = ra.astype(ra_ref.dtype)
    rank_q = (ra * qd_ref[...]).astype(bf16)
    rank_v = (ra * vd_ref[...]).astype(bf16)
    delta_q = mm(rank_q, b_ref[...])
    dq_ref[...] = delta_q.astype(dq_ref.dtype)
    q = (mm(x, w1_ref[:, R:R + D]) + qb_ref[...] * delta_q).astype(bf16)
    q_ref[...] = q * (HD ** -0.5)
    delta_v = mm(rank_v, b_ref[...])
    dv_ref[...] = delta_v.astype(dv_ref.dtype)
    v_ref[...] = (mm(x, w1_ref[:, R + 2 * D:]) + vb_ref[...] * delta_v).astype(bf16)
    k_ref[...] = mm(x, w1_ref[:, R + D:R + 2 * D]).astype(bf16)


def proj(lengths, x, w1, b, qd, vd, qb, vb, tm=256):
    n = x.shape[0]
    row = lambda c: pl.BlockSpec((tm, c), lambda i, *_: (i, 0))
    full = lambda a: pl.BlockSpec(a.shape, lambda i, *_: (0, 0), pipeline_mode=pl.Buffered(1))
    sd = jax.ShapeDtypeStruct
    return pl.pallas_call(
        functools.partial(proj_kernel, tm),
        grid_spec=pltpu.PrefetchScalarGridSpec(
            num_scalar_prefetch=1, grid=(n // tm,),
            in_specs=[row(D), full(w1), full(b)] + [full(a) for a in (qd, vd, qb, vb)],
            out_specs=[row(R), row(D), row(D), row(D), row(D), row(D),
                       pl.BlockSpec((8, R), lambda i, *_: (0, 0))]),
        out_shape=[sd((n, R), bf16), sd((n, D), bf16), sd((n, D), bf16), sd((n, D), bf16),
                   sd((n, D), bf16), sd((n, D), bf16), sd((8, R), f32)],
        name="proj",
        compiler_params=vm(48),
    )(lengths, x, w1, b, qd, vd, qb, vb)


def attn_fwd_kernel(len_ref, q_ref, k_ref, v_ref, ctx_ref, p_ref):
    s = pl.program_id(0)
    length = len_ref[s]
    live = lax.broadcasted_iota(jnp.int32, (L, 1), 0) < length
    lane = lax.broadcasted_iota(jnp.int32, (L, 2 * HD), 1)
    q = q_ref[...]
    k = k_ref[...]
    v = v_ref[...]
    zero = jnp.zeros_like(k)
    vt = v.T
    parts = []
    for h in range(2):
        kh = jnp.where((lane // HD) == h, k, zero)
        st = mm_t(kh, q)
        st = jnp.where(live, st, neg_fill)
        top = jnp.max(st, axis=0, keepdims=True)
        e = jnp.exp(st - top)
        total = jnp.sum(e, axis=0, keepdims=True)
        pt = (e * (1.0 / total)).astype(bf16)
        p_ref[h] = pt
        parts.append(mm(vt[h * HD:(h + 1) * HD], pt))
    ctx_ref[...] = jnp.concatenate(parts, axis=0).astype(bf16).T


def attn_fwd(lengths, q, k, v):
    n = q.shape[0]
    seqs = n // L
    pairs = H // 2
    blk = pl.BlockSpec((L, 2 * HD), lambda s, h, *_: (s, h))
    sd = jax.ShapeDtypeStruct
    return pl.pallas_call(
        attn_fwd_kernel,
        grid_spec=pltpu.PrefetchScalarGridSpec(
            num_scalar_prefetch=1, grid=(seqs, pairs),
            in_specs=[blk, blk, blk],
            out_specs=[blk, pl.BlockSpec((2, L, L), lambda s, h, *_: (s * pairs + h, 0, 0))]),
        out_shape=[sd((n, D), bf16), sd((seqs * H, L, L), bf16)],
        name="attn_fwd",
        compiler_params=vm(48),
    )(lengths, q, k, v)


def ffn_kernel(tm, cj, len_ref, x_ref, ctx_ref, cot_ref, w2_ref, wd_ref, g1_ref, g2_ref,
               out_ref, gh1_ref, gctx_ref, dg_ref, acc_ref):
    i = pl.program_id(0)
    n_j = FF // cj
    g1 = g1_ref[...]
    g2 = g2_ref[...]
    h1 = x_ref[...].astype(f32) + mm(ctx_ref[...], w2_ref[:, :D])
    c1 = h1 - jnp.mean(h1, axis=-1, keepdims=True)
    r1 = lax.rsqrt(jnp.mean(c1 * c1, axis=-1, keepdims=True) + eps_norm)
    y1 = c1 * r1
    x1 = y1 * g1
    x_low = x1.astype(bf16)
    acc_ref[...] = x1

    def fwd(j, carry):
        wu = w2_ref[:, pl.ds(pl.multiple_of(D + j * cj, 128), cj)]
        pre = mm(x_low, wu)
        cdf = 0.5 + 0.5 * lax.erf(pre * (0.5 ** 0.5))
        pdf = jnp.exp(pre * pre * -0.5) * 0.3989422804014327
        act = (pre * cdf).astype(bf16)
        dg_ref[j] = (cdf + pre * pdf).astype(bf16)
        acc_ref[...] += mm(act, wd_ref[pl.ds(pl.multiple_of(j * cj, 128), cj), :])
        return carry

    lax.fori_loop(0, n_j, fwd, 0)
    h2 = acc_ref[...]
    c2 = h2 - jnp.mean(h2, axis=-1, keepdims=True)
    r2 = lax.rsqrt(jnp.mean(c2 * c2, axis=-1, keepdims=True) + eps_norm)
    y2 = c2 * r2
    out_ref[...] = (y2 * g2).astype(bf16)
    per_seq = L // tm
    length = len_ref[i // per_seq]
    pos = (i % per_seq) * tm + lax.broadcasted_iota(jnp.int32, (tm, 1), 0)
    live = (pos < length).astype(f32)
    gy = cot_ref[...].astype(f32) * live * g2
    gh2 = (gy - jnp.mean(gy, axis=-1, keepdims=True)
           - y2 * jnp.mean(gy * y2, axis=-1, keepdims=True)) * r2
    g_ffn = gh2.astype(bf16)
    acc_ref[...] = gh2

    def bwd(j, carry):
        wd = wd_ref[pl.ds(pl.multiple_of(j * cj, 128), cj), :]
        g_act = mm_t(g_ffn, wd)
        g_pre = (dg_ref[j].astype(f32) * g_act).astype(bf16)
        wu = w2_ref[:, pl.ds(pl.multiple_of(D + j * cj, 128), cj)]
        acc_ref[...] += mm_t(g_pre, wu)
        return carry

    lax.fori_loop(0, n_j, bwd, 0)
    gx1 = acc_ref[...]
    gy1 = gx1 * g1
    gh1 = (gy1 - jnp.mean(gy1, axis=-1, keepdims=True)
           - y1 * jnp.mean(gy1 * y1, axis=-1, keepdims=True)) * r1
    gh1_ref[...] = gh1
    gctx_ref[...] = mm_t(gh1.astype(bf16), w2_ref[:, :D]).astype(bf16)


def ffn(lengths, x, ctx, cot, w2, wd, g1, g2, tm=256, cj=768):
    n = x.shape[0]
    row = pl.BlockSpec((tm, D), lambda i, *_: (i, 0))
    full = lambda a: pl.BlockSpec(a.shape, lambda i, *_: (0, 0), pipeline_mode=pl.Buffered(1))
    sd = jax.ShapeDtypeStruct
    return pl.pallas_call(
        functools.partial(ffn_kernel, tm, cj),
        grid_spec=pltpu.PrefetchScalarGridSpec(
            num_scalar_prefetch=1, grid=(n // tm,),
            in_specs=[row, row, row, full(w2), full(wd), full(g1), full(g2)],
            out_specs=[row, row, row],
            scratch_shapes=[pltpu.VMEM((FF // cj, tm, cj), bf16), pltpu.VMEM((tm, D), f32)]),
        out_shape=[sd((n, D), bf16), sd((n, D), f32), sd((n, D), bf16)],
        name="ffn",
        compiler_params=vm(56),
    )(lengths, x, ctx, cot, w2, wd, g1, g2)


def attn_bwd_kernel(q_ref, k_ref, v_ref, ctx_ref, gc_ref, p_ref, gq_ref, gk_ref, gv_ref):
    lane = lax.broadcasted_iota(jnp.int32, (L, 2 * HD), 1)
    q = q_ref[...]
    k = k_ref[...]
    v = v_ref[...]
    gc = gc_ref[...]
    zero = jnp.zeros_like(k)
    prod = (gc.astype(f32) * ctx_ref[...].astype(f32)).T
    kt = k.T
    gq_parts = []
    gk = jnp.zeros((L, 2 * HD), f32)
    gv = jnp.zeros((L, 2 * HD), f32)
    for h in range(2):
        mine = (lane // HD) == h
        vh = jnp.where(mine, v, zero)
        qh = jnp.where(mine, q, zero)
        gch = jnp.where(mine, gc, zero)
        pt = p_ref[h]
        gpt = mm_t(vh, gc)
        row = jnp.sum(prod[h * HD:(h + 1) * HD], axis=0, keepdims=True)
        gst = (pt.astype(f32) * (gpt - row)).astype(bf16)
        gq_parts.append(mm(kt[h * HD:(h + 1) * HD], gst))
        gk += mm(gst, qh)
        gv += mm(pt, gch)
    gq = jnp.concatenate(gq_parts, axis=0) * (HD ** -0.5)
    gq_ref[...] = gq.astype(bf16).T
    gk_ref[...] = gk.astype(bf16)
    gv_ref[...] = gv.astype(bf16)


def attn_bwd(q, k, v, ctx, gc, p):
    n = q.shape[0]
    seqs = n // L
    pairs = H // 2
    blk = pl.BlockSpec((L, 2 * HD), lambda s, h: (s, h))
    sd = jax.ShapeDtypeStruct
    return pl.pallas_call(
        attn_bwd_kernel,
        grid=(seqs, pairs),
        in_specs=[blk] * 5 + [pl.BlockSpec((2, L, L), lambda s, h: (s * pairs + h, 0, 0))],
        out_specs=[blk] * 3,
        out_shape=[sd((n, D), bf16)] * 3,
        name="attn_bwd",
        compiler_params=vm(48),
    )(q, k, v, ctx, gc, p)


def grads_kernel(gq_ref, gk_ref, gv_ref, dq_ref, dv_ref, ra_ref, gh1_ref, w1_ref, b_ref,
                 qd_ref, vd_ref, qb_ref, vb_ref, gt_ref, sqd_ref, svd_ref, sqb_ref, svb_ref):
    i = pl.program_id(0)

    @pl.when(i == 0)
    def _():
        for ref in (sqd_ref, svd_ref, sqb_ref, svb_ref):
            ref[...] = jnp.zeros_like(ref)

    gq = gq_ref[...].astype(f32)
    gv = gv_ref[...].astype(f32)
    ra = ra_ref[...].astype(f32)
    sqb_ref[...] += fold8(gq * dq_ref[...].astype(f32))
    svb_ref[...] += fold8(gv * dv_ref[...].astype(f32))
    t_q = mm_t((qb_ref[...] * gq).astype(bf16), b_ref[...])
    t_v = mm_t((vb_ref[...] * gv).astype(bf16), b_ref[...])
    sqd_ref[...] += fold8(t_q * ra)
    svd_ref[...] += fold8(t_v * ra)
    g_rank = (t_q * qd_ref[...] + t_v * vd_ref[...]).astype(bf16)
    acc = gh1_ref[...].astype(f32)
    acc += mm_t(gq_ref[...], w1_ref[:, R:R + D])
    acc += mm_t(gk_ref[...], w1_ref[:, R + D:R + 2 * D])
    acc += mm_t(gv_ref[...], w1_ref[:, R + 2 * D:])
    acc += mm_t(g_rank, w1_ref[:, :R])
    gt_ref[...] = acc.astype(bf16)


def grads(gq, gk, gv, dq, dv, ra, gh1, w1, b, qd, vd, qb, vb, tm=256):
    n = gq.shape[0]
    row = lambda c: pl.BlockSpec((tm, c), lambda i: (i, 0))
    full = lambda a: pl.BlockSpec(a.shape, lambda i: (0, 0), pipeline_mode=pl.Buffered(1))
    acc = lambda c: pl.BlockSpec((8, c), lambda i: (0, 0))
    sd = jax.ShapeDtypeStruct
    return pl.pallas_call(
        grads_kernel,
        grid=(n // tm,),
        in_specs=[row(D)] * 5 + [row(R), row(D), full(w1), full(b)] + [full(a) for a in (qd, vd, qb, vb)],
        out_specs=[row(D), acc(R), acc(R), acc(D), acc(D)],
        out_shape=[sd((n, D), bf16), sd((8, R), f32), sd((8, R), f32), sd((8, D), f32), sd((8, D), f32)],
        name="grads",
        compiler_params=vm(48),
    )(gq, gk, gv, dq, dv, ra, gh1, w1, b, qd, vd, qb, vb)


def shards(
    tokens,
    lengths,
    cotangent,
    w_query,
    w_key,
    w_value,
    w_out,
    w_up,
    w_down,
    shared_a,
    shared_b,
    gain_one,
    gain_two,
    query_d,
    query_b,
    value_d,
    value_b,
):
    axes = ("dp", "fsdp")
    seqs = tokens.shape[0]
    x = tokens.reshape(seqs * L, D)
    cot = cotangent.reshape(seqs * L, D)
    gather = lambda a: lax.all_gather(a, axes, axis=0, tiled=True)
    w1 = gather(jnp.concatenate([shared_a, w_query, w_key, w_value], axis=1))
    b = gather(shared_b)
    w2 = gather(jnp.concatenate([w_out, w_up], axis=1))
    wd = gather(w_down)
    g1, g2, qd, qb, vd, vb = (
        a.reshape(1, -1) for a in (gain_one, gain_two, query_d, query_b, value_d, value_b)
    )
    ra, dq, dv, q, k, v, sq = proj(lengths, x, w1, b, qd, vd, qb, vb)
    ctx, p = attn_fwd(lengths, q, k, v)
    out, gh1, gc = ffn(lengths, x, ctx, cot, w2, wd, g1, g2)
    gq, gk, gv = attn_bwd(q, k, v, ctx, gc, p)
    gt, s_qd, s_vd, s_qb, s_vb = grads(gq, gk, gv, dq, dv, ra, gh1, w1, b, qd, vd, qb, vb)
    count = jnp.sum(lengths).astype(f32)
    sums = tuple(jnp.sum(a, axis=0) for a in (s_qd, s_qb, s_vd, s_vb, sq))
    s_qd, s_qb, s_vd, s_vb, sq, count = lax.psum(sums + (count,), axes)
    return (out.reshape(seqs, L, D), gt.reshape(seqs, L, D), s_qd, s_qb, s_vd, s_vb, sq / count)


def solution(mesh):
    from jax.sharding import PartitionSpec as P

    both = ("dp", "fsdp")
    mat = P(both, None)
    big = P(both, None, None)
    in_specs = (big, P(both), big) + (mat,) * 8 + (P(),) * 6
    out_specs = (big, big) + (P(),) * 5
    return jax.shard_map(shards, mesh=mesh, in_specs=in_specs, out_specs=out_specs, check_vma=False)
```

time: 935 us -> 398 us (0.43); the launches traced: 920 us -> 397 us
  matrix products: 380 us -> 0 us
  Pallas kernels: 0 us -> 115 us
  local copies, waits for them, and re-layouts: 112 us -> 11.4 us
  waiting for transfers between devices: 301 us -> 210 us
  other arithmetic: 52 us -> 5.78 us
  loops' own time: 18.5 us -> 0 us
    dot_general x188 -> x0, matrix products: 380 us -> none  [the longest x11 89.1 us: dot_plain(): return jnp.dot(left, right, preferred_element_type=jnp.float32)]
    pallas_call x0 -> x5, Pallas kernels: none -> 115 us  [the longest x1 45.5 us: ffn(): pl.pallas_call(functools.partial(ffn_kernel, tm, cj), grid_spec=pltpu.Pre...]
    all_gather x8 -> x4, waiting for transfers between devices: 296 us -> 208 us  [shards(): gather = lambda a: lax.all_gather(a, axes, axis=0, tiled=True)]
    reshape x15 -> x4, local copies, waits for them, and re-layouts: 38.1 us -> 3.91 us  [shards(): a.reshape(1, -1)]
    dynamic_update_slice x24 -> x0, local copies, waits for them, and re-layouts: 31.9 us -> none  [shards(): lax.map(attend_block, (q_heads, k_heads, v_heads, key_live))]
    reduce_sum x32 -> x6, other arithmetic: 22.1 us -> 1.36 us  [the longest x1 1.29 us: shards(): count = jnp.sum(lengths).astype(f32)]
    another operation x4 -> x0, loops' own time: 18.5 us -> none  [the longest x1 14.6 us: shards(): lax.map(attend_block, (q_heads, k_heads, v_heads, key_live))]
    gt x48 -> x0, other arithmetic: 18.4 us -> none  [the longest x24 17.7 us: attend_back(): scores = jnp.where(live_keys[None, :] > 0, scores, neg_fill)]
  transfers between devices with their start and end apart: 8 -> 4, of which waited for: 6 -> 4; matrix products, arithmetic and copies ran while one was open for 17% -> 2% of each run, Pallas kernels for 0% -> 9%
where the time goes in v1:
time: 398 us; the launch traced here: 397 us
  waiting for transfers between devices  210 us (53%)
  Pallas kernels  115 us (29%)
  blocking collectives  40 us (10%)
  between operations  14.5 us (4%)
  local copies, waits for them, and re-layouts  11.4 us (3%)
  other arithmetic  5.78 us (1%)
    all_gather x4, waiting for transfers between devices, shards(): gather = lambda a: lax.all_gather(a, axes, axis=0, tiled=True)  208 us
    pallas_call x1, Pallas kernels, ffn(): pl.pallas_call(functools.partial(ffn_kernel, tm, cj), grid_spec=pltpu.Pre...  45.5 us
    psum x1, blocking collectives, shards(): s_qd, s_qb, s_vd, s_vb, sq, count = lax.psum(sums + (count,), axes)  40 us
    pallas_call x1, Pallas kernels, attn_fwd(): pl.pallas_call(attn_fwd_kernel, grid_spec=pltpu.PrefetchScalarGridSpec(nu...  20.4 us
    pallas_call x1, Pallas kernels, attn_bwd(): pl.pallas_call(attn_bwd_kernel, grid=(seqs, pairs), in_specs=[blk] * 5 +...  19.4 us
    pallas_call x1, Pallas kernels, proj(): pl.pallas_call(functools.partial(proj_kernel, tm), grid_spec=pltpu.Prefet...  16 us
    pallas_call x1, Pallas kernels, grads(): pl.pallas_call(grads_kernel, grid=(n // tm,), in_specs=[row(D)] * 5 + [ro...  14.1 us
  transfers between devices with their start and end apart: 4, of which 4 were waited for; matrix products, arithmetic and copies ran while one was open for 2% of the time, Pallas kernels for 9%

profile of v1, /device:TPU:0, one launch (start us, length us, event | category | flops | bytes accessed | tf_op | source)
XLA Modules:
  0.0 396.8 jit_solution(14033366521030886157)
XLA Ops:
  7.2 0.0 all-gather.7.cloned.1.call-start
  7.2 0.7 all-gather.7.cloned.1.call-update
  7.9 0.0 all-gather.5.cloned.1.call-start
  7.9 1.5 pad_maximum_fusion.1
  9.5 0.0 all-gather.5.cloned.1.call-update
  9.5 0.0 all-gather.11.cloned.1.call-start
  9.6 0.7 all-gather.11.cloned.1.call-update
  10.2 0.0 all-gather.9.cloned.1.call-start
  10.3 1.6 pad_maximum_fusion
  11.9 0.0 all-gather.9.cloned.1.call-update
  11.9 1.3 reduce_sum.59
  13.9 0.7 reshape.47.qb_ref
  14.6 0.7 reshape.48.vb_ref
  15.2 1.3 reshape.50.g1_ref
  16.5 1.3 reshape.51.g2_ref
  17.8 50.8 %all-gather.7.cloned.1.call-done.b_ref = bf16[1024,768]{1,0:T(8,128)(2,1)} async-done(((bf16[32,768]{1,0:T(8,128)(2,1)}), bf16[1024,768]{1,0:T(8,128)(2,1)}) %all-gather.7.cloned.1.call-update) | async-done | bytes 1572880 | tf_op jit(solution)/shard_map/all_gather | solution.py:315
  68.6 67.1 %all-gather.5.cloned.1.call-done.w1_ref = bf16[768,3328]{1,0:T(8,128)(2,1)} async-done(((bf16[24,3328]{1,0:T(8,128)(2,1)}), bf16[768,3328]{1,0:T(8,128)(2,1)}) %all-gather.5.cloned.1.call-update) | async-done | bytes 5111824 | tf_op jit(solution)/shard_map/all_gather | solution.py:315
  135.7 0.0 copy-start.5
  135.7 0.7 copy-done.5
  136.4 0.0 copy-start.7
  136.4 0.7 copy-done.7
  137.1 0.0 copy-start.9
  137.1 0.7 copy-done.9
  137.7 0.0 copy-start.10
  137.7 16.0 %proj.1 = (bf16[1024,1024]{1,0:T(8,128)(2,1)}, bf16[1024,768]{1,0:T(8,128)(2,1)S(1)}, bf16[1024,768]{1,0:T(8,128)(2,1)S(1)}, bf16[1024,768]{1,0:T(8,128)(2,1)S(1...) custom-call(s32[2]{0:T(128)S(1)} %copy-done.9, bf16[1024,768]{1,0:T(8,128)(2,1)} %bitcast.10, ...), custom_call_target="tpu_custom_call" | custom-call | tf_op jit(solution)/shard_map/proj/pallas_call | solution.py:70
  153.7 0.0 copy-start.3
  153.7 1.1 copy-done.3
  154.8 0.0 copy-start.4
  154.8 1.2 copy-done.4
  156.0 0.0 copy-start
  156.0 0.0 copy-done.10
  156.0 0.0 copy-start.1
  156.1 2.0 copy-done.1
  158.0 20.4 %attn_fwd.1 = (bf16[1024,768]{1,0:T(8,128)(2,1)S(1)}, bf16[24,512,512]{2,1,0:T(8,128)(2,1)}) custom-call(s32[2]{0:T(128)S(1)} %copy-done.10, bf16[1024,768]{1,0:T(8,128)(2,1)S(1)} %get-tuple-element.27.q_ref, bf16[1024,768]{1,0:T(8,128)(2,1)S(1)} %copy-done.1, bf16[1024,768]{1,0:T(8,128)(2,1)} %get-tuple-element.29.v_ref), custom_call_target="tpu_custom_call" | custom-call | tf_op jit(solution)/shard_map/attn_fwd/pallas_call | solution.py:114
  178.4 0.0 copy-done
  178.4 0.0 copy-start.2
  178.4 1.1 copy-done.2
  179.6 21.1 %all-gather.11.cloned.1.call-done.wd_ref = bf16[3072,768]{1,0:T(8,128)(2,1)} async-done(((bf16[96,768]{1,0:T(8,128)(2,1)}), bf16[3072,768]{1,0:T(8,128)(2,1)}) %all-gather.11.cloned.1.call-update) | async-done | bytes 4718608 | tf_op jit(solution)/shard_map/all_gather | solution.py:315
  200.7 69.3 %all-gather.9.cloned.1.call-done.w2_ref = bf16[768,3840]{1,0:T(8,128)(2,1)} async-done(((bf16[24,3840]{1,0:T(8,128)(2,1)}), bf16[768,3840]{1,0:T(8,128)(2,1)}) %all-gather.9.cloned.1.call-update) | async-done | bytes 5898256 | tf_op jit(solution)/shard_map/all_gather | solution.py:315
  270.0 45.5 %ffn.1 = (bf16[1024,768]{1,0:T(8,128)(2,1)}, f32[1024,768]{1,0:T(8,128)}, bf16[1024,768]{1,0:T(8,128)(2,1)}) custom-call(s32[2]{0:T(128)} %len_ref.5, bf16[1024,768]{1,0:T(8,128)(2,1)} %bitcast.11, bf16[1024,768]{1,0:T(8,128)(2,1)} %copy-done.2, bf16[1024,768]{1,0:T(8,128)(2,1)} %bitcast.12, bf16[768,3840]{1,0:T(8,128)(2,1)} %all-gather.9.cloned.1.call-done.w2_ref, ...), custom_call_target="tpu_custom_call" | custom-call | tf_op jit(solution)/shard_map/ffn/pallas_call | solution.py:188
  315.4 0.0 copy-start.6
  315.4 0.0 copy-start.8
  315.4 19.4 %attn_bwd.1 = (bf16[1024,768]{1,0:T(8,128)(2,1)S(1)}, bf16[1024,768]{1,0:T(8,128)(2,1)S(1)}, bf16[1024,768]{1,0:T(8,128)(2,1)S(1)}) custom-call(bf16[1024,768]{1,0:T(8,128)(2,1)} %copy-done, bf16[1024,768]{1,0:T(8,128)(2,1)} %get-tuple-element.28.k_ref, bf16[1024,768]{1,0:T(8,128)(2,1)} %get-tuple-element.29.v_ref, bf16[1024,768]{1,0:T(8,128)(2,1)} %copy-done.2, ...), custom_call_target="tpu_custom_call" | custom-call | tf_op jit(solution)/shard_map/attn_bwd/pallas_call | solution.py:237
  334.8 0.0 copy-done.6
  334.9 0.0 copy-done.8
  334.9 14.1 %grads.1 = (bf16[1024,768]{1,0:T(8,128)(2,1)}, f32[8,1024]{1,0:T(8,128)S(1)}, f32[8,1024]{1,0:T(8,128)S(1)}, f32[8,768]{1,0:T(8,128)S(1)}, f32[8,768]{1,0:T(8,128)S(1)}) custom-call(bf16[1024,768]{1,0:T(8,128)(2,1)S(1)} %get-tuple-element.34.gq_ref, bf16[1024,768]{1,0:T(8,128)(2,1)S(1)} %get-tuple-element.35.gk_ref, ...), custom_call_target="tpu_custom_call" | custom-call | tf_op jit(solution)/shard_map/grads/pallas_call | solution.py:281
  349.0 40.0 %all-reduce = (f32[1024]{0:T(1024)}, f32[768]{0:T(1024)}, f32[1024]{0:T(1024)}, f32[768]{0:T(1024)}, f32[1024]{0:T(1024)S(1)}, /*index=5*/f32[]{:T(128)}) all-reduce(f32[1024]{0:T(1024)S(1)} %reduce_sum.54, f32[768]{0:T(1024)S(1)} %reduce_sum.55, f32[1024]{0:T(1024)S(1)} %reduce_sum.56, ...), channel_id=1, replica_groups=mesh['dp'=8,'fsdp'=4] {'dp','fsdp'}, use_global_device_ids=true, to_apply=%region_1.0 | all-reduce | flops 4609 | bytes 36872 | tf_op jit(solution)/shard_map/psum | solution.py:330
  389.0 1.3 broadcast_divide_fusion
  (5 shorter events, 0.1 us)
Async XLA Ops:
  7.2 61.4 %all-gather.7.cloned.1.call-start = ((), (), s32[]{:S(2)}) async-start(), calls=%async_computation.1 | async-start | bytes 1622016 | tf_op jit(solution)/shard_map/all_gather | solution.py:315
  7.9 127.8 %all-gather.5.cloned.1.call-start = ((), (), s32[]{:S(2)}) async-start(), calls=%async_computation | async-start | bytes 5271552 | tf_op jit(solution)/shard_map/all_gather | solution.py:315
  9.5 191.2 %all-gather.11.cloned.1.call-start = ((), (), s32[]{:S(2)}) async-start(), calls=%async_computation.3 | async-start | bytes 4866048 | tf_op jit(solution)/shard_map/all_gather | solution.py:315
  10.2 259.7 %all-gather.9.cloned.1.call-start = ((), (), s32[]{:S(2)}) async-start(), calls=%async_computation.2 | async-start | bytes 6082560 | tf_op jit(solution)/shard_map/all_gather | solution.py:315
  135.7 0.7 copy-start.5
  136.4 0.7 copy-start.7
  137.1 0.7 copy-start.9
  137.7 18.3 %copy-start.10 = (s32[2]{0:T(128)S(1)}, s32[2]{0:T(128)}, u32[]{:S(2)}) copy-start(s32[2]{0:T(128)} %len_ref.5) | copy-start | bytes 28
  153.7 1.1 copy-start.3
  154.8 1.2 copy-start.4
  156.0 22.4 %copy-start = (bf16[1024,768]{1,0:T(8,128)(2,1)}, bf16[1024,768]{1,0:T(8,128)(2,1)S(1)}, u32[]{:S(2)}) copy-start(bf16[1024,768]{1,0:T(8,128)(2,1)S(1)} %get-tuple-element.27.q_ref) | copy-start | bytes 4718596
  156.0 2.0 copy-start.1
  178.4 1.1 copy-start.2
  315.4 19.4 %copy-start.6 = (f32[1024]{0:T(1024)S(1)}, f32[1024]{0:T(1024)}, u32[]{:S(2)}) copy-start(f32[1024]{0:T(1024)} %param.30) | copy-start | bytes 12292
  315.4 19.4 %copy-start.8 = (f32[1024]{0:T(1024)S(1)}, f32[1024]{0:T(1024)}, u32[]{:S(2)}) copy-start(f32[1024]{0:T(1024)} %param.32) | copy-start | bytes 12292
Sparse Core Ops, SparseCore 0:
  10.9 57.6 all-gather.6
  72.0 63.7 all-gather.4
  138.5 62.1 all-gather.10
  203.9 66.0 all-gather.8

commit v2 on v1

--- a/solution.py
+++ b/solution.py
@@ -289,6 +289,238 @@
     )(gq, gk, gv, dq, dv, ra, gh1, w1, b, qd, vd, qb, vb)
 
 
+MESH = pl.DeviceIdType.MESH
+N_COPIES = 31
+
+
+def flip(i, bit):
+    if bit == 0:
+        return i
+    if bit == 1:
+        return i + 1 - 2 * lax.rem(i, 2)
+    if bit == 2:
+        return lax.rem(i + 2, 4)
+    return 3 - i
+
+
+class Gather:
+    def __init__(self, srcs, dsts, send, recv, local):
+        self.srcs, self.dsts, self.send, self.recv, self.local = srcs, dsts, send, recv, local
+        dp = lax.axis_index("dp")
+        self.z = lax.axis_index("fsdp")
+        self.core = lax.rem(dp, 2)
+        self.chip = dp // 2
+
+    def peers(self):
+        chip, core, z = self.chip, self.core, self.z
+        out = [(chip * 2 + 1 - core, z), (flip(chip, 1) * 2 + core, z), (flip(chip, 2) * 2 + core, z)]
+        return out + [(chip * 2 + core, flip(z, j)) for j in (1, 2, 3)]
+
+    def barrier(self):
+        sem = pltpu.get_barrier_semaphore()
+        for peer in self.peers():
+            pl.semaphore_signal(sem, inc=1, device_id=peer, device_id_type=MESH)
+        pl.semaphore_wait(sem, 6)
+
+    def block(self, a, k, j, core):
+        rows = self.srcs[a].shape[0]
+        at = ((flip(self.chip, k) * 2 + core) * 4 + flip(self.z, j)) * rows
+        return self.dsts[a].at[pl.ds(pl.multiple_of(at, 8), rows), :]
+
+    def z_route(self, j):
+        return j - 1, 0, j, (self.chip * 2 + self.core, flip(self.z, j))
+
+    def side_route(self, axis, j):
+        peer = (flip(self.chip, axis) * 2 + self.core, self.z)
+        return 3 + 4 * (axis - 1) + j, axis, j, peer
+
+    def far_route(self, j):
+        axis = 2 if j % 2 == 0 else 1
+        return 11 + j, 3, j, (flip(self.chip, axis) * 2 + self.core, self.z)
+
+    def pair_route(self, k, j):
+        return 15 + 4 * k + j, k, j, (self.chip * 2 + 1 - self.core, self.z)
+
+    def copy(self, a, route, src, dst):
+        key, _, _, peer = route
+        return pltpu.make_async_remote_copy(
+            src_ref=src, dst_ref=dst, send_sem=self.send.at[a, key], recv_sem=self.recv.at[a, key],
+            device_id=peer, device_id_type=MESH)
+
+    def start(self, route, k, j, own=False):
+        for a in range(len(self.srcs)):
+            here = self.block(a, k, j, self.core)
+            self.copy(a, route, self.srcs[a] if own else here, here).start()
+
+    def arrive(self, route):
+        _, k, j, _ = route
+        for a in range(len(self.srcs)):
+            core = 1 - self.core if route[0] >= 15 else self.core
+            here = self.block(a, k, j, core)
+            self.copy(a, route, here, here).wait_recv()
+
+    def keep_own(self, a):
+        return pltpu.make_async_copy(self.srcs[a], self.block(a, 0, 0, self.core), self.local.at[a])
+
+    def first(self):
+        for axis in (1, 2):
+            self.start(self.side_route(axis, 0), 0, 0, own=True)
+        for j in (1, 2, 3):
+            self.start(self.z_route(j), 0, 0, own=True)
+        self.start(self.pair_route(0, 0), 0, 0, own=True)
+        for a in range(len(self.srcs)):
+            self.keep_own(a).start()
+
+    def take_z(self, j):
+        self.arrive(self.z_route(j))
+        for axis in (1, 2):
+            self.start(self.side_route(axis, j), 0, j)
+        self.start(self.pair_route(0, j), 0, j)
+
+    def take_side(self, axis, j):
+        self.arrive(self.side_route(axis, j))
+        if axis == (1 if j % 2 == 0 else 2):
+            self.start(self.far_route(j), axis, j)
+        self.start(self.pair_route(axis, j), axis, j)
+
+    def take_far(self, j):
+        self.arrive(self.far_route(j))
+        self.start(self.pair_route(3, j), 3, j)
+
+    def last(self):
+        for k in range(4):
+            for j in range(4):
+                self.arrive(self.pair_route(k, j))
+        for a in range(len(self.srcs)):
+            self.keep_own(a).wait()
+            for j in (1, 2, 3):
+                self.done(a, self.z_route(j))
+            for j in range(4):
+                for axis in (1, 2):
+                    self.done(a, self.side_route(axis, j))
+                self.done(a, self.far_route(j))
+                for k in range(4):
+                    self.done(a, self.pair_route(k, j))
+
+    def done(self, a, route):
+        here = self.block(a, 0, 0, self.core)
+        self.copy(a, route, here, here).wait_send()
+
+    def events(self):
+        z = lambda j: functools.partial(self.take_z, j)
+        s = lambda axis, j: functools.partial(self.take_side, axis, j)
+        d = lambda j: functools.partial(self.take_far, j)
+        return [self.barrier, self.first, s(1, 0), s(2, 0), z(1), z(2), s(1, 1), s(2, 1), z(3), d(0), s(1, 2), s(2, 2),
+                d(1), s(1, 3), s(2, 3), d(2), d(3), self.last]
+
+
+def gather_scratch(n):
+    return [pltpu.SemaphoreType.DMA((n, N_COPIES)), pltpu.SemaphoreType.DMA((n, N_COPIES)),
+            pltpu.SemaphoreType.DMA((n,))]
+
+
+def gather_kernel(n, *refs):
+    g = Gather(refs[:n], refs[n:2 * n], *refs[2 * n:])
+    for event in g.events():
+        event()
+
+
+def gather(arrays, collective_id):
+    axes = ("dp", "fsdp")
+    n_dp, n_z = lax.axis_size("dp"), lax.axis_size("fsdp")
+    if (n_dp, n_z) != (8, 4) or any(a.shape[0] % 8 for a in arrays):
+        return [lax.all_gather(a, axes, axis=0, tiled=True) for a in arrays]
+    n = len(arrays)
+    whole = [jax.ShapeDtypeStruct((a.shape[0] * n_dp * n_z,) + a.shape[1:], a.dtype) for a in arrays]
+    spec = pl.BlockSpec(memory_space=pl.ANY)
+    return pl.pallas_call(
+        functools.partial(gather_kernel, n),
+        in_specs=[spec] * n,
+        out_specs=[spec] * n,
+        out_shape=whole,
+        scratch_shapes=gather_scratch(n),
+        name="gather",
+        compiler_params=pltpu.CompilerParams(collective_id=collective_id, has_side_effects=True),
+    )(*arrays)
+
+
+def total_kernel(n_z, n_chip, len_ref, sqd_ref, svd_ref, sq_ref, sqb_ref, svb_ref,
+                 qd_out, qb_out, vd_out, vb_out, stat_out,
+                 mine, pair, line, plane, sends, pair_sem, line_sem, plane_sem):
+    dp, z = lax.axis_index("dp"), lax.axis_index("fsdp")
+    core, chip = lax.rem(dp, 2), dp // 2
+    partner = (chip * 2 + 1 - core, z)
+    lines = [(dp, lax.rem(z + j, n_z)) for j in range(1, n_z)]
+    planes = [(lax.rem(chip + j, n_chip) * 2 + core, z) for j in range(1, n_chip)]
+    sem = pltpu.get_barrier_semaphore()
+    for peer in [partner] + lines + planes:
+        pl.semaphore_signal(sem, inc=1, device_id=peer, device_id_type=MESH)
+
+    mine[...] = jnp.zeros_like(mine)
+    for row, ref in enumerate((sqd_ref, svd_ref, sq_ref, sqb_ref, svb_ref)):
+        mine[row:row + 1, :ref.shape[1]] = jnp.sum(ref[...], axis=0, keepdims=True)
+    count = len_ref[0]
+    for s in range(1, len_ref.shape[0]):
+        count += len_ref[s]
+    mine[5:6, :] = jnp.full((1, R), count.astype(f32))
+    pl.semaphore_wait(sem, n_z + n_chip - 1)
+
+    def send(src, dst, at, recv, peer):
+        return pltpu.make_async_remote_copy(
+            src_ref=src, dst_ref=dst, send_sem=sends.at[at], recv_sem=recv, device_id=peer, device_id_type=MESH)
+
+    swap = send(mine, pair, 0, pair_sem, partner)
+    swap.start()
+    swap.wait_recv()
+    line[z] = mine[...] + pair[...]
+    out = [send(line.at[z], line.at[z], j, line_sem.at[j - 1], lines[j - 1]) for j in range(1, n_z)]
+    for copy in out:
+        copy.start()
+    for j in range(1, n_z):
+        came = lax.rem(z + n_z - j, n_z)
+        send(line.at[came], line.at[came], j, line_sem.at[j - 1], lines[j - 1]).wait_recv()
+    total = line[0]
+    for i in range(1, n_z):
+        total += line[i]
+    plane[chip] = total
+    far = [send(plane.at[chip], plane.at[chip], n_z - 1 + j, plane_sem.at[j - 1], planes[j - 1])
+           for j in range(1, n_chip)]
+    for copy in far:
+        copy.start()
+    for j in range(1, n_chip):
+        came = lax.rem(chip + n_chip - j, n_chip)
+        send(plane.at[came], plane.at[came], n_z - 1 + j, plane_sem.at[j - 1], planes[j - 1]).wait_recv()
+    total = plane[0]
+    for i in range(1, n_chip):
+        total += plane[i]
+    qd_out[...] = total[0:1]
+    vd_out[...] = total[1:2]
+    stat_out[...] = total[2:3] / total[5:6]
+    qb_out[...] = total[3:4, :D]
+    vb_out[...] = total[4:5, :D]
+    for copy in [swap] + out + far:
+        copy.wait_send()
+
+
+def total(lengths, s_qd, s_vd, sq, s_qb, s_vb, collective_id):
+    n_z = lax.axis_size("fsdp")
+    n_chip = lax.axis_size("dp") // 2
+    vmem = pl.BlockSpec(memory_space=pltpu.VMEM)
+    sd = jax.ShapeDtypeStruct
+    dma = pltpu.SemaphoreType.DMA
+    return pl.pallas_call(
+        functools.partial(total_kernel, n_z, n_chip),
+        in_specs=[pl.BlockSpec(memory_space=pltpu.SMEM)] + [vmem] * 5,
+        out_specs=[vmem] * 5,
+        out_shape=[sd((1, R), f32), sd((1, D), f32), sd((1, R), f32), sd((1, D), f32), sd((1, R), f32)],
+        scratch_shapes=[pltpu.VMEM((8, R), f32), pltpu.VMEM((8, R), f32), pltpu.VMEM((n_z, 8, R), f32),
+                        pltpu.VMEM((n_chip, 8, R), f32), dma((n_z + n_chip - 1,)), dma(()), dma((n_z - 1,)),
+                        dma((n_chip - 1,))],
+        name="total",
+        compiler_params=pltpu.CompilerParams(collective_id=collective_id, has_side_effects=True),
+    )(lengths, s_qd, s_vd, sq, s_qb, s_vb)
+
+
 def shards(
     tokens,
     lengths,
@@ -308,15 +540,18 @@
     value_d,
     value_b,
 ):
-    axes = ("dp", "fsdp")
     seqs = tokens.shape[0]
     x = tokens.reshape(seqs * L, D)
     cot = cotangent.reshape(seqs * L, D)
-    gather = lambda a: lax.all_gather(a, axes, axis=0, tiled=True)
-    w1 = gather(jnp.concatenate([shared_a, w_query, w_key, w_value], axis=1))
-    b = gather(shared_b)
-    w2 = gather(jnp.concatenate([w_out, w_up], axis=1))
-    wd = gather(w_down)
+    w1, b, w2, wd = gather(
+        (
+            jnp.concatenate([shared_a, w_query, w_key, w_value], axis=1),
+            shared_b,
+            jnp.concatenate([w_out, w_up], axis=1),
+            w_down,
+        ),
+        0,
+    )
     g1, g2, qd, qb, vd, vb = (
         a.reshape(1, -1) for a in (gain_one, gain_two, query_d, query_b, value_d, value_b)
     )
@@ -325,10 +560,8 @@
     out, gh1, gc = ffn(lengths, x, ctx, cot, w2, wd, g1, g2)
     gq, gk, gv = attn_bwd(q, k, v, ctx, gc, p)
     gt, s_qd, s_vd, s_qb, s_vb = grads(gq, gk, gv, dq, dv, ra, gh1, w1, b, qd, vd, qb, vb)
-    count = jnp.sum(lengths).astype(f32)
-    sums = tuple(jnp.sum(a, axis=0) for a in (s_qd, s_qb, s_vd, s_vb, sq))
-    s_qd, s_qb, s_vd, s_vb, sq, count = lax.psum(sums + (count,), axes)
-    return (out.reshape(seqs, L, D), gt.reshape(seqs, L, D), s_qd, s_qb, s_vd, s_vb, sq / count)
+    sums = total(lengths, s_qd, s_vd, sq, s_qb, s_vb, 1)
+    return (out.reshape(seqs, L, D), gt.reshape(seqs, L, D)) + tuple(a.reshape(-1) for a in sums)
 
 
 def solution(mesh):

time: 398 us -> 247 us (0.62)
  waiting for transfers between devices: 210 us -> 0 us
  Pallas kernels: 115 us -> 222 us
  blocking collectives: 40 us -> 0 us
  between operations: 14.5 us -> 0.71 us
  local copies, waits for them, and re-layouts: 11.4 us -> 17.7 us
    all_gather x4 -> x0, waiting for transfers between devices: 208 us -> none  [shards(): gather = lambda a: lax.all_gather(a, axes, axis=0, tiled=True)]
    pallas_call x0 -> x2, Pallas kernels: none -> 107 us  [the longest x1 94.3 us: gather(): pl.pallas_call(functools.partial(gather_kernel, n), in_specs=[spec] * n,...]
    psum x1 -> x0, blocking collectives: 40 us -> none  [shards(): s_qd, s_qb, s_vd, s_vb, sq, count = lax.psum(sums + (count,), axes)]
    unnamed x22 -> x33, local copies, waits for them, and re-layouts: 7.44 us -> 13.8 us
  transfers between devices with their start and end apart: 4 -> 0, of which waited for: 4 -> 0; matrix products, arithmetic and copies ran while one was open for 2% -> 0% of each run, Pallas kernels for 9% -> 0%
where the time goes in v2:
time: 247 us; the launch traced here: 246 us
  Pallas kernels  222 us (90%)
  local copies, waits for them, and re-layouts  17.7 us (7%)
  other arithmetic  5.69 us (2%)
    pallas_call x1, Pallas kernels, gather(): pl.pallas_call(functools.partial(gather_kernel, n), in_specs=[spec] * n,...  94.3 us
    pallas_call x1, Pallas kernels, ffn(): pl.pallas_call(functools.partial(ffn_kernel, tm, cj), grid_spec=pltpu.Pre...  45.5 us
    pallas_call x1, Pallas kernels, attn_fwd(): pl.pallas_call(attn_fwd_kernel, grid_spec=pltpu.PrefetchScalarGridSpec(nu...  20.4 us
    pallas_call x1, Pallas kernels, attn_bwd(): pl.pallas_call(attn_bwd_kernel, grid=(seqs, pairs), in_specs=[blk] * 5 +...  19.4 us
    pallas_call x1, Pallas kernels, proj(): pl.pallas_call(functools.partial(proj_kernel, tm), grid_spec=pltpu.Prefet...  16 us
    pallas_call x1, Pallas kernels, grads(): pl.pallas_call(grads_kernel, grid=(n // tm,), in_specs=[row(D)] * 5 + [ro...  14.1 us
    unnamed x33, local copies, waits for them, and re-layouts  13.8 us
    pallas_call x1, Pallas kernels, total(): pl.pallas_call(functools.partial(total_kernel, n_z, n_chip), in_specs=[pl...  12.4 us

profile of v2, /device:TPU:0, one launch (start us, length us, event | category | flops | bytes accessed | tf_op | source)
XLA Modules:
  0.0 246.1 jit_solution(386981625691603077)
XLA Ops:
  0.6 0.7 reshape.62.qb_ref
  1.3 0.7 reshape.63.vb_ref
  2.0 1.3 reshape.65.g1_ref
  3.3 1.3 reshape.66.g2_ref
  4.5 1.5 pad_maximum_fusion.1.refs_0_
  6.1 1.6 pad_maximum_fusion.refs_2_
  7.7 94.3 %gather.1 = (bf16[768,3328]{1,0:T(8,128)(2,1)}, bf16[1024,768]{1,0:T(8,128)(2,1)}, bf16[768,3840]{1,0:T(8,128)(2,1)}, bf16[3072,768]{1,0:T(8,128)(2,1)}) custom-call(bf16[24,3328]{1,0:T(8,128)(2,1)} %pad_maximum_fusion.1.refs_0_, bf16[32,768]{1,0:T(8,128)(2,1)} %refs_1_.1, bf16[24,3840]{1,0:T(8,128)(2,1)} %pad_maximum_fusion.refs_2_, bf16[96,768]{1,0:T(8,128)(2,1)} %refs_3_.1), custom_call_target="tpu_custom_call" | custom-call | tf_op jit(solution)/shard_map/gather/pallas_call | solution.py:436
  102.0 0.0 copy-start.10
  102.0 0.7 copy-done.10
  102.6 0.0 copy-start.12
  102.7 0.7 copy-done.12
  103.3 0.0 copy-start.14
  103.3 0.7 copy-done.14
  104.0 16.0 %proj.1 = (bf16[1024,1024]{1,0:T(8,128)(2,1)}, bf16[1024,768]{1,0:T(8,128)(2,1)S(1)}, bf16[1024,768]{1,0:T(8,128)(2,1)S(1)}, bf16[1024,768]{1,0:T(8,128)(2,1)S(1...) custom-call(s32[2]{0:T(128)S(1)} %copy-done.14, bf16[1024,768]{1,0:T(8,128)(2,1)} %bitcast.13, ...), custom_call_target="tpu_custom_call" | custom-call | tf_op jit(solution)/shard_map/proj/pallas_call | solution.py:70
  120.0 0.0 copy-start.3
  120.0 1.1 copy-done.3
  121.1 0.0 copy-start.4
  121.1 1.2 copy-done.4
  122.3 0.0 copy-start
  122.3 0.0 copy-start.5
  122.3 0.0 copy-start.1
  122.3 2.0 copy-done.1
  124.3 20.4 %attn_fwd.1 = (bf16[1024,768]{1,0:T(8,128)(2,1)S(1)}, bf16[24,512,512]{2,1,0:T(8,128)(2,1)}) custom-call(s32[2]{0:T(128)S(1)} %copy-done.14, bf16[1024,768]{1,0:T(8,128)(2,1)S(1)} %get-tuple-element.38.q_ref, bf16[1024,768]{1,0:T(8,128)(2,1)S(1)} %copy-done.1, bf16[1024,768]{1,0:T(8,128)(2,1)} %get-tuple-element.40.v_ref), custom_call_target="tpu_custom_call" | custom-call | tf_op jit(solution)/shard_map/attn_fwd/pallas_call | solution.py:114
  144.7 0.0 copy-done
  144.7 0.0 copy-done.5
  144.7 0.0 copy-start.2
  144.7 1.2 copy-done.2
  145.9 45.5 %ffn.1 = (bf16[1024,768]{1,0:T(8,128)(2,1)}, f32[1024,768]{1,0:T(8,128)}, bf16[1024,768]{1,0:T(8,128)(2,1)}) custom-call(s32[2]{0:T(128)} %len_ref.7, bf16[1024,768]{1,0:T(8,128)(2,1)} %bitcast.14, bf16[1024,768]{1,0:T(8,128)(2,1)} %copy-done.2, bf16[1024,768]{1,0:T(8,128)(2,1)} %bitcast.15, bf16[768,3840]{1,0:T(8,128)(2,1)} %get-tuple-element.42.w2_ref, ...), custom_call_target="tpu_custom_call" | custom-call | tf_op jit(solution)/shard_map/ffn/pallas_call | solution.py:188
  191.4 0.0 copy-start.11
  191.4 0.0 copy-start.13
  191.4 19.4 %attn_bwd.1 = (bf16[1024,768]{1,0:T(8,128)(2,1)S(1)}, bf16[1024,768]{1,0:T(8,128)(2,1)S(1)}, bf16[1024,768]{1,0:T(8,128)(2,1)S(1)}) custom-call(bf16[1024,768]{1,0:T(8,128)(2,1)} %copy-done, bf16[1024,768]{1,0:T(8,128)(2,1)} %get-tuple-element.39.k_ref, bf16[1024,768]{1,0:T(8,128)(2,1)} %get-tuple-element.40.v_ref, bf16[1024,768]{1,0:T(8,128)(2,1)} %copy-done.2, ...), custom_call_target="tpu_custom_call" | custom-call | tf_op jit(solution)/shard_map/attn_bwd/pallas_call | solution.py:237
  210.8 0.0 copy-done.11
  210.8 0.0 copy-done.13
  210.8 14.1 %grads.1 = (bf16[1024,768]{1,0:T(8,128)(2,1)}, f32[8,1024]{1,0:T(8,128)S(1)}, f32[8,1024]{1,0:T(8,128)S(1)}, f32[8,768]{1,0:T(8,128)S(1)}, f32[8,768]{1,0:T(8,128)S(1)}) custom-call(bf16[1024,768]{1,0:T(8,128)(2,1)S(1)} %get-tuple-element.47.gq_ref, bf16[1024,768]{1,0:T(8,128)(2,1)S(1)} %get-tuple-element.48.gk_ref, ...), custom_call_target="tpu_custom_call" | custom-call | tf_op jit(solution)/shard_map/grads/pallas_call | solution.py:281
  224.9 0.0 copy-start.6
  224.9 0.6 copy-done.6
  225.5 0.0 copy-start.7
  225.5 0.6 copy-done.7
  226.1 0.0 copy-start.8
  226.1 0.6 copy-done.8
  226.7 0.0 copy-start.9
  226.7 0.6 copy-done.9
  227.3 12.4 %total.1 = (f32[1,1024]{1,0:T(1,128)}, f32[1,768]{1,0:T(1,128)}, f32[1,1024]{1,0:T(1,128)}, f32[1,768]{1,0:T(1,128)}, f32[1,1024]{1,0:T(1,128)}) custom-call(s32[2]{0:T(128)} %len_ref.7, f32[8,1024]{1,0:T(8,128)} %copy-done.6, f32[8,1024]{1,0:T(8,128)} %copy-done.7, f32[8,1024]{1,0:T(8,128)} %copy-done.5, f32[8,768]{1,0:T(8,128)} %copy-done.8, ...), custom_call_target="tpu_custom_call" | custom-call | tf_op jit(solution)/shard_map/total/pallas_call | solution.py:511
  239.7 1.3 reduce
  241.0 1.3 reduce.1
  242.3 1.3 copy.27
  243.6 1.3 copy.28
  244.8 1.3 copy.29
Async XLA Ops:
  102.0 0.7 copy-start.10
  102.6 0.7 copy-start.12
  103.3 0.7 copy-start.14
  120.0 1.1 copy-start.3
  121.1 1.2 copy-start.4
  122.3 22.4 %copy-start = (bf16[1024,768]{1,0:T(8,128)(2,1)}, bf16[1024,768]{1,0:T(8,128)(2,1)S(1)}, u32[]{:S(2)}) copy-start(bf16[1024,768]{1,0:T(8,128)(2,1)S(1)} %get-tuple-element.38.q_ref) | copy-start | bytes 4718596
  122.3 22.4 %copy-start.5 = (f32[8,1024]{1,0:T(8,128)}, f32[8,1024]{1,0:T(8,128)S(1)}, u32[]{:S(2)}) copy-start(f32[8,1024]{1,0:T(8,128)S(1)} %get-tuple-element.57.sq_ref) | copy-start | bytes 98308
  122.3 2.0 copy-start.1
  144.7 1.2 copy-start.2
  191.4 19.4 %copy-start.11 = (f32[1024]{0:T(1024)S(1)}, f32[1024]{0:T(1024)}, u32[]{:S(2)}) copy-start(f32[1024]{0:T(1024)} %param.30) | copy-start | bytes 12292
  191.4 19.4 %copy-start.13 = (f32[1024]{0:T(1024)S(1)}, f32[1024]{0:T(1024)}, u32[]{:S(2)}) copy-start(f32[1024]{0:T(1024)} %param.32) | copy-start | bytes 12292
  224.9 0.6 copy-start.6
  225.5 0.6 copy-start.7
  226.1 0.6 copy-start.8
  226.7 0.6 copy-start.9
